TPU v7x, 256 devices: a whole 4x4x8 slice. The times are simulated.
256 devices in a mesh: row: 16 (over z, core), col: 16 (over y, x).
Axes of the slice: x: 4, y: 4, z: 8, core: 2. Of those that a mesh axis runs over, the one named last changes fastest.
Arguments:
- blocks: bfloat16 [16, 16, 5, 128, 8192], P('row', 'col'), may hold values from -6 to 6
- coords: int32 [16, 16, 5, 3], P('row', 'col'), may hold values from 0 to 15, as said below
- counts: int32 [16, 16], P('row', 'col'), may hold values from 1 to 5, as said below
- doc_factor: bfloat16 [32768, 128], P(('col', 'row')), may hold values from -6 to 6
- ctx_factor: bfloat16 [512, 128], P('col'), may hold values from -0.0625 to 0.0625
Outputs:
- mttkrp: float32 [32768, 128], P(('row', 'col'))
Inputs may be any that keep to these rules, and one draw needn't show every extreme that they name: coords[..., 0] lies in 0 to 15, coords[..., 1] in 0 to 15, coords[..., 2] in 0 to 7; slots at or past the device's count are ignored. `counts`: some device uses all 5 slots.
All inputs are finite; a program needn't handle non-finite values.
Results may differ from a plain program's by a relative error of at most 0.0029.
Values may be sent and summed in bfloat16 or wider, within the bound.
No kernel may reach another device: no remote copies, remote signals or barrier semaphores. Data moves between devices by JAX's collectives and lax.ppermute only.
A program may use at most 64 MiB of HBM per device.

v0:
```python
import jax
import jax.numpy as jnp
from jax import lax
from jax.sharding import PartitionSpec as P

BQ = 128
BD = 128
BK = 64
QBC = 1


def kr_table(brows, crows):
    table = brows[:, None, :].astype(jnp.float32) * crows[None, :, :].astype(jnp.float32)
    return table.reshape(brows.shape[0] * crows.shape[0], brows.shape[1]).astype(jnp.bfloat16)


def body(blocks, coords, counts, doc_factor, ctx_factor):
    doc_slab = lax.all_gather(doc_factor, "row", axis=0, tiled=True)
    ctx_all = lax.all_gather(ctx_factor, "col", axis=0, tiled=True)
    own_blocks = blocks[0, 0]
    own_coords = coords[0, 0]
    used = counts[0, 0]
    rank = doc_slab.shape[1]
    dev_rows = QBC * BQ
    all_rows = dev_rows * lax.axis_size("col")
    start = jnp.int32(0)
    empty = jnp.zeros((all_rows, rank), jnp.float32)

    def step(index, acc):
        place = own_coords[index]
        qstart = place[0] * BQ
        inside = jnp.logical_and(qstart >= start, qstart < start + all_rows)

        def add_term(inner):
            brows = lax.dynamic_slice_in_dim(doc_slab, place[1] * BD, BD, 0)
            crows = lax.dynamic_slice_in_dim(ctx_all, place[2] * BK, BK, 0)
            term = jnp.dot(
                own_blocks[index], kr_table(brows, crows), preferred_element_type=jnp.float32
            )
            local = jnp.clip(qstart, 0, all_rows - BQ)
            current = lax.dynamic_slice_in_dim(inner, local, BQ, 0)
            return lax.dynamic_update_slice_in_dim(inner, current + term, local, 0)

        return lax.cond(inside, add_term, lambda inner: inner, acc)

    partial_value = lax.fori_loop(0, used, step, empty)
    return lax.psum_scatter(partial_value, "col", scatter_dimension=0, tiled=True)


def solution(mesh):
    placed = (
        P("row", "col", None, None, None),
        P("row", "col", None, None),
        P("row", "col"),
        P(("col", "row"), None),
        P("col", None),
    )
    return jax.shard_map(
        body, mesh=mesh, in_specs=placed, out_specs=P(("row", "col"), None), check_vma=False
    )
```

profile of v0, /device:TPU:2, one launch (start us, length us, event | category | flops | bytes accessed | tf_op | source)
XLA Modules:
  0.0 172.4 jit_solution(1418539375337259537)
XLA Ops:
  6.5 23.0 %all_gather.6 = bf16[2048,128]{1,0:T(8,128)(2,1)} all-gather(bf16[128,128]{1,0:T(8,128)(2,1)} %param.12), channel_id=1, replica_groups=mesh['row'=16,'col'=16] {'row'}, dimensions={0}, use_global_device_ids=true | all-gather | bytes 557056 | tf_op jit(solution)/shard_map/all_gather | solution.py:18
  29.6 23.7 %all_gather.7 = bf16[512,128]{1,0:T(8,128)(2,1)S(1)} all-gather(bf16[32,128]{1,0:T(8,128)(2,1)} %param.13), channel_id=1, replica_groups=mesh['row'=16,'col'=16] {'col'}, dimensions={0}, use_global_device_ids=true | all-gather | bytes 139264 | tf_op jit(solution)/shard_map/all_gather | solution.py:19
  53.3 0.8 copy.7
  54.1 35.4 %while.13 = (s32[]{:T(128)}, f32[2048,128]{1,0:T(8,128)S(1)}, s32[]{:T(128)}, s32[5,3]{1,0:T(8,128)S(1)}, bf16[5,128,8192]{2,1,0:T(8,128)(2,1)}, /*index=5*/bf16...) while((s32[]{:T(128)}, f32[2048,128]{1,0:T(8,128)S(1)}, ...), condition=%wide.region_3.4_spmd, body=%wide.region_0.3_spmd.sunk | while | flops 270573568 | bytes 6799827 | solution.py:46
  54.9 6.2 %conditional.2 = (f32[2048,128]{1,0:T(8,128)S(1)}) conditional(s32[]{:T(128)} %convert_element_type.27, f32[2048,128]{1,0:T(8,128)S(1)} %get-tuple-element.150, (s32[]{:T(128)}, f32[2048,128]{1,0:T(8,128)S(1)}, s32[]{:T(128)}, bf16[5,128,8192]{2,1,0:T(8,128)(2,1)}, s32[1,3]{1,0:T(1,128)S(1)}, /*index=5*/bf16[2048,128]{1,0:T(8,128)(2,1)}, ...), branch_computations={%region_1.0_spmd, %region_2.2_spmd} | conditional | flops 270573568 | bytes 6799554 | solution.py:44
  54.9 0.6 fusion.7
  56.1 0.8 dynamic-slice_convert_fusion
  57.6 0.6 multiply_convert_fusion
  58.2 2.3 %fusion.3 = f32[128,128]{1,0:T(8,128)S(1)} fusion(bf16[8192,128]{1,0:T(8,128)(2,1)S(1)} %bitcast.18, bf16[5,128,8192]{2,1,0:T(8,128)(2,1)} %get-tuple-element.54, s32[]{:T(128)S(6)} %select_n.2, f32[2048,128]{1,0:T(8,128)S(1)} %get-tuple-element.52, s32[]{:T(128)S(6)} %min.3), kind=kOutput, calls=%fused_computation.4 | convolution fusion | flops 268451840 | bytes 4325384 | tf_op jit(solution)/shard_map/while/body/cond/branch_1_fun/dot_general | solution.py:37
  60.5 0.6 dynamic_update_slice.2
  61.8 6.2 %conditional.2 = (f32[2048,128]{1,0:T(8,128)S(1)}) conditional(s32[]{:T(128)} %convert_element_type.27, f32[2048,128]{1,0:T(8,128)S(1)} %get-tuple-element.150, (s32[]{:T(128)}, f32[2048,128]{1,0:T(8,128)S(1)}, s32[]{:T(128)}, bf16[5,128,8192]{2,1,0:T(8,128)(2,1)}, s32[1,3]{1,0:T(1,128)S(1)}, /*index=5*/bf16[2048,128]{1,0:T(8,128)(2,1)}, ...), branch_computations={%region_1.0_spmd, %region_2.2_spmd} | conditional | flops 270573568 | bytes 6799554 | solution.py:44
  61.8 0.6 fusion.7
  63.1 0.8 dynamic-slice_convert_fusion
  64.5 0.6 multiply_convert_fusion
  65.2 2.3 %fusion.3 = f32[128,128]{1,0:T(8,128)S(1)} fusion(bf16[8192,128]{1,0:T(8,128)(2,1)S(1)} %bitcast.18, bf16[5,128,8192]{2,1,0:T(8,128)(2,1)} %get-tuple-element.54, s32[]{:T(128)S(6)} %select_n.2, f32[2048,128]{1,0:T(8,128)S(1)} %get-tuple-element.52, s32[]{:T(128)S(6)} %min.3), kind=kOutput, calls=%fused_computation.4 | convolution fusion | flops 268451840 | bytes 4325384 | tf_op jit(solution)/shard_map/while/body/cond/branch_1_fun/dot_general | solution.py:37
  68.8 6.2 %conditional.2 = (f32[2048,128]{1,0:T(8,128)S(1)}) conditional(s32[]{:T(128)} %convert_element_type.27, f32[2048,128]{1,0:T(8,128)S(1)} %get-tuple-element.150, (s32[]{:T(128)}, f32[2048,128]{1,0:T(8,128)S(1)}, s32[]{:T(128)}, bf16[5,128,8192]{2,1,0:T(8,128)(2,1)}, s32[1,3]{1,0:T(1,128)S(1)}, /*index=5*/bf16[2048,128]{1,0:T(8,128)(2,1)}, ...), branch_computations={%region_1.0_spmd, %region_2.2_spmd} | conditional | flops 270573568 | bytes 6799554 | solution.py:44
  68.8 0.6 fusion.7
  70.0 0.8 dynamic-slice_convert_fusion
  71.5 0.6 multiply_convert_fusion
  72.1 2.3 %fusion.3 = f32[128,128]{1,0:T(8,128)S(1)} fusion(bf16[8192,128]{1,0:T(8,128)(2,1)S(1)} %bitcast.18, bf16[5,128,8192]{2,1,0:T(8,128)(2,1)} %get-tuple-element.54, s32[]{:T(128)S(6)} %select_n.2, f32[2048,128]{1,0:T(8,128)S(1)} %get-tuple-element.52, s32[]{:T(128)S(6)} %min.3), kind=kOutput, calls=%fused_computation.4 | convolution fusion | flops 268451840 | bytes 4325384 | tf_op jit(solution)/shard_map/while/body/cond/branch_1_fun/dot_general | solution.py:37
  75.7 6.2 %conditional.2 = (f32[2048,128]{1,0:T(8,128)S(1)}) conditional(s32[]{:T(128)} %convert_element_type.27, f32[2048,128]{1,0:T(8,128)S(1)} %get-tuple-element.150, (s32[]{:T(128)}, f32[2048,128]{1,0:T(8,128)S(1)}, s32[]{:T(128)}, bf16[5,128,8192]{2,1,0:T(8,128)(2,1)}, s32[1,3]{1,0:T(1,128)S(1)}, /*index=5*/bf16[2048,128]{1,0:T(8,128)(2,1)}, ...), branch_computations={%region_1.0_spmd, %region_2.2_spmd} | conditional | flops 270573568 | bytes 6799554 | solution.py:44
  75.7 0.6 fusion.7
  77.0 0.8 dynamic-slice_convert_fusion
  78.4 0.6 multiply_convert_fusion
  79.1 2.3 %fusion.3 = f32[128,128]{1,0:T(8,128)S(1)} fusion(bf16[8192,128]{1,0:T(8,128)(2,1)S(1)} %bitcast.18, bf16[5,128,8192]{2,1,0:T(8,128)(2,1)} %get-tuple-element.54, s32[]{:T(128)S(6)} %select_n.2, f32[2048,128]{1,0:T(8,128)S(1)} %get-tuple-element.52, s32[]{:T(128)S(6)} %min.3), kind=kOutput, calls=%fused_computation.4 | convolution fusion | flops 268451840 | bytes 4325384 | tf_op jit(solution)/shard_map/while/body/cond/branch_1_fun/dot_general | solution.py:37
  82.7 6.2 %conditional.2 = (f32[2048,128]{1,0:T(8,128)S(1)}) conditional(s32[]{:T(128)} %convert_element_type.27, f32[2048,128]{1,0:T(8,128)S(1)} %get-tuple-element.150, (s32[]{:T(128)}, f32[2048,128]{1,0:T(8,128)S(1)}, s32[]{:T(128)}, bf16[5,128,8192]{2,1,0:T(8,128)(2,1)}, s32[1,3]{1,0:T(1,128)S(1)}, /*index=5*/bf16[2048,128]{1,0:T(8,128)(2,1)}, ...), branch_computations={%region_1.0_spmd, %region_2.2_spmd} | conditional | flops 270573568 | bytes 6799554 | solution.py:44
  82.7 0.6 fusion.7
  83.9 0.8 dynamic-slice_convert_fusion
  85.4 0.6 multiply_convert_fusion
  86.0 2.3 %fusion.3 = f32[128,128]{1,0:T(8,128)S(1)} fusion(bf16[8192,128]{1,0:T(8,128)(2,1)S(1)} %bitcast.18, bf16[5,128,8192]{2,1,0:T(8,128)(2,1)} %get-tuple-element.54, s32[]{:T(128)S(6)} %select_n.2, f32[2048,128]{1,0:T(8,128)S(1)} %get-tuple-element.52, s32[]{:T(128)S(6)} %min.3), kind=kOutput, calls=%fused_computation.4 | convolution fusion | flops 268451840 | bytes 4325384 | tf_op jit(solution)/shard_map/while/body/cond/branch_1_fun/dot_general | solution.py:37
  89.6 1.0 copy-done
  90.5 75.0 %reduce-scatter.2.cloned.1.call-done = f32[128,128]{1,0:T(8,128)} async-done(((f32[2048,128]{1,0:T(8,128)}), f32[128,128]{1,0:T(8,128)}) %reduce-scatter.2.cloned.1.call-update) | async-done | bytes 65552 | tf_op jit(solution)/shard_map/reduce_scatter | solution.py:47
  (18 shorter events, 2.5 us)
Async XLA Ops:
  6.5 159.0 %reduce-scatter.2.cloned.1.call-start = ((), (), s32[]{:S(2)}) async-start(), calls=%async_computation.1 | async-start | bytes 1114112 | tf_op jit(solution)/shard_map/reduce_scatter | solution.py:47
  89.5 1.0 copy-start
Sparse Core Ops, SparseCore 0:
  90.7 74.8 reduce-scatter.1
where the time goes:
time: 173 us; the launch traced here: 172 us
  waiting for transfers between devices  75 us (43%)
  blocking collectives  46.8 us (27%)
  between operations  13.4 us (8%)
  matrix products  11.5 us (7%)
  loops' own time  10.9 us (6%)
  local copies, waits for them, and re-layouts  7.87 us (5%)
  other arithmetic  7 us (4%)
    reduce_scatter x1, waiting for transfers between devices, body(): lax.psum_scatter(partial_value, 'col', scatter_dimension=0, tiled=True)  75 us
    all_gather x1, blocking collectives, body(): ctx_all = lax.all_gather(ctx_factor, 'col', axis=0, tiled=True)  23.7 us
    all_gather x1, blocking collectives, body(): doc_slab = lax.all_gather(doc_factor, 'row', axis=0, tiled=True)  23 us
    dot_general x5, matrix products, add_term(): jnp.dot(own_blocks[index], kr_table(brows, crows), preferred_element_type...  11.5 us
    another operation x5, loops' own time, step(): return lax.cond(inside, add_term, lambda inner: inner, acc)  6.59 us
    another operation x1, loops' own time, body(): partial_value = lax.fori_loop(0, used, step, empty)  4.29 us
    convert_element_type x5, other arithmetic, kr_table(): brows[:, None, :].astype(jnp.float32)  3.84 us
  transfers between devices with their start and end apart: 1, of which 1 were waited for; matrix products, arithmetic and copies ran while one was open for 0% of the time, Pallas kernels for 0%

commit v1 on v0

--- a/solution.py
+++ b/solution.py
@@ -9,6 +9,27 @@
 QBC = 1
 
 
+def collect(x, axis, dim):
+    count, index, extent = (lax.axis_size(axis), lax.axis_index(axis), x.shape[dim])
+    ahead = [(i, (i + 1) % count) for i in range(count)]
+    backward = [(i, (i - 1) % count) for i in range(count)]
+    out = jnp.zeros((*x.shape[:dim], count * extent, *x.shape[dim + 1 :]), x.dtype)
+    out = lax.dynamic_update_slice_in_dim(out, x, index * extent, axis=dim)
+    from_left = from_right = x
+    half = count // 2
+    for turn in range(1, half + 1):
+        from_left = lax.ppermute(from_left, axis, ahead)
+        out = lax.dynamic_update_slice_in_dim(
+            out, from_left, (index - turn) % count * extent, axis=dim
+        )
+        if turn < count - half:
+            from_right = lax.ppermute(from_right, axis, backward)
+            out = lax.dynamic_update_slice_in_dim(
+                out, from_right, (index + turn) % count * extent, axis=dim
+            )
+    return out
+
+
 def kr_table(brows, crows):
     table = brows[:, None, :].astype(jnp.float32) * crows[None, :, :].astype(jnp.float32)
     return table.reshape(brows.shape[0] * crows.shape[0], brows.shape[1]).astype(jnp.bfloat16)
@@ -16,7 +37,7 @@
 
 def body(blocks, coords, counts, doc_factor, ctx_factor):
     doc_slab = lax.all_gather(doc_factor, "row", axis=0, tiled=True)
-    ctx_all = lax.all_gather(ctx_factor, "col", axis=0, tiled=True)
+    ctx_all = collect(ctx_factor, "col", 0)
     own_blocks = blocks[0, 0]
     own_coords = coords[0, 0]
     used = counts[0, 0]

time: 173 us -> 200 us (1.16)
  starting transfers between devices: 0.01 us -> 32.9 us
  blocking collectives: 46.8 us -> 22.8 us
  waiting for transfers between devices: 75 us -> 92.2 us
    ppermute x0 -> x15, starting transfers between devices: none -> 32.9 us  [the longest x7 29.9 us: collect(): from_right = lax.ppermute(from_right, axis, backward)]
    all_gather x1 -> x0, blocking collectives: 23.7 us -> none  [body(): ctx_all = lax.all_gather(ctx_factor, 'col', axis=0, tiled=True)]
    ppermute x0 -> x15, waiting for transfers between devices: none -> 16.5 us  [the longest x8 16.5 us: collect(): from_left = lax.ppermute(from_left, axis, ahead)]
  transfers between devices with their start and end apart: 1 -> 16, of which waited for: 1 -> 8; matrix products, arithmetic and copies ran while one was open for 0% -> 1% of each run, Pallas kernels for 0% -> 0%
where the time goes in v1:
time: 200 us
  waiting for transfers between devices  92.2 us (46%)
  starting transfers between devices  32.9 us (16%)
  blocking collectives  22.8 us (11%)
  between operations  13.4 us (7%)
  matrix products  11.5 us (6%)
  loops' own time  11.1 us (6%)
  local copies, waits for them, and re-layouts  8.79 us (4%)
  other arithmetic  7 us (4%)
    reduce_scatter x1, waiting for transfers between devices, body(): lax.psum_scatter(partial_value, 'col', scatter_dimension=0, tiled=True)  75.7 us
    ppermute x7, starting transfers between devices, collect(): from_right = lax.ppermute(from_right, axis, backward)  29.9 us
    all_gather x1, blocking collectives, body(): doc_slab = lax.all_gather(doc_factor, 'row', axis=0, tiled=True)  22.8 us
    ppermute x8, waiting for transfers between devices, collect(): from_left = lax.ppermute(from_left, axis, ahead)  16.5 us
    dot_general x5, matrix products, add_term(): jnp.dot(own_blocks[index], kr_table(brows, crows), preferred_element_type...  11.5 us
    another operation x5, loops' own time, step(): return lax.cond(inside, add_term, lambda inner: inner, acc)  6.76 us
    another operation x1, loops' own time, body(): partial_value = lax.fori_loop(0, used, step, empty)  4.29 us
  transfers between devices with their start and end apart: 16, of which 8 were waited for; matrix products, arithmetic and copies ran while one was open for 1% of the time, Pallas kernels for 0%

profile of v1, /device:TPU:2, one launch (start us, length us, event | category | flops | bytes accessed | tf_op | source)
XLA Modules:
  0.0 199.7 jit_solution(2360566166202746300)
XLA Ops:
  6.5 1.5 collective-permute-start
  8.8 22.8 %all_gather.3 = bf16[2048,128]{1,0:T(8,128)(2,1)} all-gather(bf16[128,128]{1,0:T(8,128)(2,1)} %param.12), channel_id=1, replica_groups=mesh['row'=16,'col'=16] {'row'}, dimensions={0}, use_global_device_ids=true | all-gather | bytes 557056 | tf_op jit(solution)/shard_map/all_gather | solution.py:39
  33.1 1.5 collective-permute-start.2
  34.6 2.5 %collective-permute-start.3 = (bf16[32,128]{1,0:T(8,128)(2,1)S(1)}, bf16[32,128]{1,0:T(8,128)(2,1)S(1)}, u32[]{:S(2)}, u32[]{:S(2)}) collective-permute-start(bf16[32,128]{1,0:T(8,128)(2,1)S(1)} %collective-permute-done.1), channel_id=1, source_target_pairs={{0,15},{1,0},{2,1},{3,2},{4,3},{5,4},{6,5},{7,6},{8,7},{9,8},{10,9... | collective-permute-start | bytes 24584 | tf_op jit(solution)/shard_map/ppermute | solution.py:26
  37.1 1.5 collective-permute-done.2
  38.6 5.3 %collective-permute-start.5 = (bf16[32,128]{1,0:T(8,128)(2,1)S(1)}, bf16[32,128]{1,0:T(8,128)(2,1)S(1)}, u32[]{:S(2)}, u32[]{:S(2)}) collective-permute-start(bf16[32,128]{1,0:T(8,128)(2,1)S(1)} %collective-permute-done.3), channel_id=1, source_target_pairs={{0,15},{1,0},{2,1},{3,2},{4,3},{5,4},{6,5},{7,6},{8,7},{9,8},{10,9... | collective-permute-start | bytes 24584 | tf_op jit(solution)/shard_map/ppermute | solution.py:26
  43.9 1.6 collective-permute-done.4
  45.6 5.3 %collective-permute-start.7 = (bf16[32,128]{1,0:T(8,128)(2,1)S(1)}, bf16[32,128]{1,0:T(8,128)(2,1)S(1)}, u32[]{:S(2)}, u32[]{:S(2)}) collective-permute-start(bf16[32,128]{1,0:T(8,128)(2,1)S(1)} %collective-permute-done.5), channel_id=1, source_target_pairs={{0,15},{1,0},{2,1},{3,2},{4,3},{5,4},{6,5},{7,6},{8,7},{9,8},{10,9... | collective-permute-start | bytes 24584 | tf_op jit(solution)/shard_map/ppermute | solution.py:26
  50.9 1.6 collective-permute-done.6
  52.5 5.3 %collective-permute-start.9 = (bf16[32,128]{1,0:T(8,128)(2,1)S(1)}, bf16[32,128]{1,0:T(8,128)(2,1)S(1)}, u32[]{:S(2)}, u32[]{:S(2)}) collective-permute-start(bf16[32,128]{1,0:T(8,128)(2,1)S(1)} %collective-permute-done.7), channel_id=1, source_target_pairs={{0,15},{1,0},{2,1},{3,2},{4,3},{5,4},{6,5},{7,6},{8,7},{9,8},{10,9... | collective-permute-start | bytes 24584 | tf_op jit(solution)/shard_map/ppermute | solution.py:26
  57.9 1.6 collective-permute-done.8
  59.5 5.3 %collective-permute-start.11 = (bf16[32,128]{1,0:T(8,128)(2,1)S(1)}, bf16[32,128]{1,0:T(8,128)(2,1)S(1)}, u32[]{:S(2)}, u32[]{:S(2)}) collective-permute-start(bf16[32,128]{1,0:T(8,128)(2,1)S(1)} %collective-permute-done.9), channel_id=1, source_target_pairs={{0,15},{1,0},{2,1},{3,2},{4,3},{5,4},{6,5},{7,6},{8,7},{9,8},{10,9... | collective-permute-start | bytes 24584 | tf_op jit(solution)/shard_map/ppermute | solution.py:26
  64.9 1.6 collective-permute-done.10
  66.5 5.3 %collective-permute-start.13 = (bf16[32,128]{1,0:T(8,128)(2,1)S(1)}, bf16[32,128]{1,0:T(8,128)(2,1)S(1)}, u32[]{:S(2)}, u32[]{:S(2)}) collective-permute-start(bf16[32,128]{1,0:T(8,128)(2,1)S(1)} %collective-permute-done.11), channel_id=1, source_target_pairs={{0,15},{1,0},{2,1},{3,2},{4,3},{5,4},{6,5},{7,6},{8,7},{9,8},{10,9... | collective-permute-start | bytes 24584 | tf_op jit(solution)/shard_map/ppermute | solution.py:26
  71.8 1.6 collective-permute-done.12
  73.5 6.9 %collective-permute-done.14 = bf16[32,128]{1,0:T(8,128)(2,1)S(1)} collective-permute-done((bf16[32,128]{1,0:T(8,128)(2,1)S(1)}, bf16[32,128]{1,0:T(8,128)(2,1)S(1)}, u32[]{:S(2)}, u32[]{:S(2)}) %collective-permute-start.14) | collective-permute-done | bytes 8224 | tf_op jit(solution)/shard_map/ppermute | solution.py:21
  80.5 35.6 %while.13 = (s32[]{:T(128)}, f32[2048,128]{1,0:T(8,128)S(1)}, s32[]{:T(128)}, s32[5,3]{1,0:T(8,128)S(1)}, bf16[5,128,8192]{2,1,0:T(8,128)(2,1)}, /*index=5*/bf16...) while((s32[]{:T(128)}, f32[2048,128]{1,0:T(8,128)S(1)}, ...), condition=%wide.region_3.4_spmd, body=%wide.region_0.3_spmd.sunk | while | flops 270573568 | bytes 6799827 | solution.py:67
  81.2 6.3 %conditional.2 = (f32[2048,128]{1,0:T(8,128)S(1)}) conditional(s32[]{:T(128)} %convert_element_type.27, f32[2048,128]{1,0:T(8,128)S(1)} %get-tuple-element.150, (s32[]{:T(128)}, f32[2048,128]{1,0:T(8,128)S(1)}, s32[]{:T(128)}, bf16[5,128,8192]{2,1,0:T(8,128)(2,1)}, s32[1,3]{1,0:T(1,128)S(1)}, /*index=5*/bf16[2048,128]{1,0:T(8,128)(2,1)}, ...), branch_computations={%region_1.1_spmd, %region_2.2_spmd} | conditional | flops 270573568 | bytes 6799554 | solution.py:65
  82.5 0.8 dynamic-slice_convert_fusion
  84.6 2.3 %fusion.3 = f32[128,128]{1,0:T(8,128)S(1)} fusion(bf16[8192,128]{1,0:T(8,128)(2,1)S(1)} %bitcast.18, bf16[5,128,8192]{2,1,0:T(8,128)(2,1)} %get-tuple-element.54, s32[]{:T(128)S(6)} %select_n.90, f32[2048,128]{1,0:T(8,128)S(1)} %get-tuple-element.52, s32[]{:T(128)S(6)} %min.3), kind=kOutput, calls=%fused_computation.4 | convolution fusion | flops 268451840 | bytes 4325384 | tf_op jit(solution)/shard_map/while/body/cond/branch_1_fun/dot_general | solution.py:58
  88.2 6.3 %conditional.2 = (f32[2048,128]{1,0:T(8,128)S(1)}) conditional(s32[]{:T(128)} %convert_element_type.27, f32[2048,128]{1,0:T(8,128)S(1)} %get-tuple-element.150, (s32[]{:T(128)}, f32[2048,128]{1,0:T(8,128)S(1)}, s32[]{:T(128)}, bf16[5,128,8192]{2,1,0:T(8,128)(2,1)}, s32[1,3]{1,0:T(1,128)S(1)}, /*index=5*/bf16[2048,128]{1,0:T(8,128)(2,1)}, ...), branch_computations={%region_1.1_spmd, %region_2.2_spmd} | conditional | flops 270573568 | bytes 6799554 | solution.py:65
  89.5 0.8 dynamic-slice_convert_fusion
  91.6 2.3 %fusion.3 = f32[128,128]{1,0:T(8,128)S(1)} fusion(bf16[8192,128]{1,0:T(8,128)(2,1)S(1)} %bitcast.18, bf16[5,128,8192]{2,1,0:T(8,128)(2,1)} %get-tuple-element.54, s32[]{:T(128)S(6)} %select_n.90, f32[2048,128]{1,0:T(8,128)S(1)} %get-tuple-element.52, s32[]{:T(128)S(6)} %min.3), kind=kOutput, calls=%fused_computation.4 | convolution fusion | flops 268451840 | bytes 4325384 | tf_op jit(solution)/shard_map/while/body/cond/branch_1_fun/dot_general | solution.py:58
  95.2 6.3 %conditional.2 = (f32[2048,128]{1,0:T(8,128)S(1)}) conditional(s32[]{:T(128)} %convert_element_type.27, f32[2048,128]{1,0:T(8,128)S(1)} %get-tuple-element.150, (s32[]{:T(128)}, f32[2048,128]{1,0:T(8,128)S(1)}, s32[]{:T(128)}, bf16[5,128,8192]{2,1,0:T(8,128)(2,1)}, s32[1,3]{1,0:T(1,128)S(1)}, /*index=5*/bf16[2048,128]{1,0:T(8,128)(2,1)}, ...), branch_computations={%region_1.1_spmd, %region_2.2_spmd} | conditional | flops 270573568 | bytes 6799554 | solution.py:65
  96.5 0.8 dynamic-slice_convert_fusion
  98.6 2.3 %fusion.3 = f32[128,128]{1,0:T(8,128)S(1)} fusion(bf16[8192,128]{1,0:T(8,128)(2,1)S(1)} %bitcast.18, bf16[5,128,8192]{2,1,0:T(8,128)(2,1)} %get-tuple-element.54, s32[]{:T(128)S(6)} %select_n.90, f32[2048,128]{1,0:T(8,128)S(1)} %get-tuple-element.52, s32[]{:T(128)S(6)} %min.3), kind=kOutput, calls=%fused_computation.4 | convolution fusion | flops 268451840 | bytes 4325384 | tf_op jit(solution)/shard_map/while/body/cond/branch_1_fun/dot_general | solution.py:58
  102.2 6.3 %conditional.2 = (f32[2048,128]{1,0:T(8,128)S(1)}) conditional(s32[]{:T(128)} %convert_element_type.27, f32[2048,128]{1,0:T(8,128)S(1)} %get-tuple-element.150, (s32[]{:T(128)}, f32[2048,128]{1,0:T(8,128)S(1)}, s32[]{:T(128)}, bf16[5,128,8192]{2,1,0:T(8,128)(2,1)}, s32[1,3]{1,0:T(1,128)S(1)}, /*index=5*/bf16[2048,128]{1,0:T(8,128)(2,1)}, ...), branch_computations={%region_1.1_spmd, %region_2.2_spmd} | conditional | flops 270573568 | bytes 6799554 | solution.py:65
  105.6 2.3 %fusion.3 = f32[128,128]{1,0:T(8,128)S(1)} fusion(bf16[8192,128]{1,0:T(8,128)(2,1)S(1)} %bitcast.18, bf16[5,128,8192]{2,1,0:T(8,128)(2,1)} %get-tuple-element.54, s32[]{:T(128)S(6)} %select_n.90, f32[2048,128]{1,0:T(8,128)S(1)} %get-tuple-element.52, s32[]{:T(128)S(6)} %min.3), kind=kOutput, calls=%fused_computation.4 | convolution fusion | flops 268451840 | bytes 4325384 | tf_op jit(solution)/shard_map/while/body/cond/branch_1_fun/dot_general | solution.py:58
  109.2 6.3 %conditional.2 = (f32[2048,128]{1,0:T(8,128)S(1)}) conditional(s32[]{:T(128)} %convert_element_type.27, f32[2048,128]{1,0:T(8,128)S(1)} %get-tuple-element.150, (s32[]{:T(128)}, f32[2048,128]{1,0:T(8,128)S(1)}, s32[]{:T(128)}, bf16[5,128,8192]{2,1,0:T(8,128)(2,1)}, s32[1,3]{1,0:T(1,128)S(1)}, /*index=5*/bf16[2048,128]{1,0:T(8,128)(2,1)}, ...), branch_computations={%region_1.1_spmd, %region_2.2_spmd} | conditional | flops 270573568 | bytes 6799554 | solution.py:65
  112.6 2.3 %fusion.3 = f32[128,128]{1,0:T(8,128)S(1)} fusion(bf16[8192,128]{1,0:T(8,128)(2,1)S(1)} %bitcast.18, bf16[5,128,8192]{2,1,0:T(8,128)(2,1)} %get-tuple-element.54, s32[]{:T(128)S(6)} %select_n.90, f32[2048,128]{1,0:T(8,128)S(1)} %get-tuple-element.52, s32[]{:T(128)S(6)} %min.3), kind=kOutput, calls=%fused_computation.4 | convolution fusion | flops 268451840 | bytes 4325384 | tf_op jit(solution)/shard_map/while/body/cond/branch_1_fun/dot_general | solution.py:58
  116.2 1.0 copy-done
  117.2 75.7 %reduce-scatter.2.cloned.1.call-done = f32[128,128]{1,0:T(8,128)} async-done(((f32[2048,128]{1,0:T(8,128)}), f32[128,128]{1,0:T(8,128)}) %reduce-scatter.2.cloned.1.call-update) | async-done | bytes 65552 | tf_op jit(solution)/shard_map/reduce_scatter | solution.py:68
  (64 shorter events, 13.3 us)
Async XLA Ops:
  6.5 186.3 %reduce-scatter.2.cloned.1.call-start = ((), (), s32[]{:S(2)}) async-start(), calls=%async_computation.1 | async-start | bytes 1114112 | tf_op jit(solution)/shard_map/reduce_scatter | solution.py:68
  6.5 26.6 %collective-permute-start = (bf16[32,128]{1,0:T(8,128)(2,1)}, bf16[32,128]{1,0:T(8,128)(2,1)S(1)}, u32[]{:S(2)}, u32[]{:S(2)}) collective-permute-start(bf16[32,128]{1,0:T(8,128)(2,1)} %param.13), channel_id=1, source_target_pairs={{0,1},{1,2},{2,3},{3,4},{4,5},{5,6},{6,7},{7,8},{8,9},{9,10},{10,1... | collective-permute-start | bytes 24584 | tf_op jit(solution)/shard_map/ppermute | solution.py:21
  8.0 26.6 %collective-permute-start.1 = (bf16[32,128]{1,0:T(8,128)(2,1)}, bf16[32,128]{1,0:T(8,128)(2,1)S(1)}, u32[]{:S(2)}, u32[]{:S(2)}) collective-permute-start(bf16[32,128]{1,0:T(8,128)(2,1)} %param.13), channel_id=1, source_target_pairs={{0,15},{1,0},{2,1},{3,2},{4,3},{5,4},{6,5},{7,6},{8,7},{9,8},{10,9... | collective-permute-start | bytes 24584 | tf_op jit(solution)/shard_map/ppermute | solution.py:26
  33.1 5.5 %collective-permute-start.2 = (bf16[32,128]{1,0:T(8,128)(2,1)S(1)}, bf16[32,128]{1,0:T(8,128)(2,1)S(1)}, u32[]{:S(2)}, u32[]{:S(2)}) collective-permute-start(bf16[32,128]{1,0:T(8,128)(2,1)S(1)} %collective-permute-done), channel_id=1, source_target_pairs={{0,1},{1,2},{2,3},{3,4},{4,5},{5,6},{6,7},{7,8},{8,9},{9,10},{10,1... | collective-permute-start | bytes 24584 | tf_op jit(solution)/shard_map/ppermute | solution.py:21
  34.6 4.0 %collective-permute-start.3 = (bf16[32,128]{1,0:T(8,128)(2,1)S(1)}, bf16[32,128]{1,0:T(8,128)(2,1)S(1)}, u32[]{:S(2)}, u32[]{:S(2)}) collective-permute-start(bf16[32,128]{1,0:T(8,128)(2,1)S(1)} %collective-permute-done.1), channel_id=1, source_target_pairs={{0,15},{1,0},{2,1},{3,2},{4,3},{5,4},{6,5},{7,6},{8,7},{9,8},{10,9... | collective-permute-start | bytes 24584 | tf_op jit(solution)/shard_map/ppermute | solution.py:26
  38.6 7.0 %collective-permute-start.4 = (bf16[32,128]{1,0:T(8,128)(2,1)S(1)}, bf16[32,128]{1,0:T(8,128)(2,1)S(1)}, u32[]{:S(2)}, u32[]{:S(2)}) collective-permute-start(bf16[32,128]{1,0:T(8,128)(2,1)S(1)} %collective-permute-done.2), channel_id=1, source_target_pairs={{0,1},{1,2},{2,3},{3,4},{4,5},{5,6},{6,7},{7,8},{8,9},{9,10},{10,1... | collective-permute-start | bytes 24584 | tf_op jit(solution)/shard_map/ppermute | solution.py:21
  38.6 7.0 %collective-permute-start.5 = (bf16[32,128]{1,0:T(8,128)(2,1)S(1)}, bf16[32,128]{1,0:T(8,128)(2,1)S(1)}, u32[]{:S(2)}, u32[]{:S(2)}) collective-permute-start(bf16[32,128]{1,0:T(8,128)(2,1)S(1)} %collective-permute-done.3), channel_id=1, source_target_pairs={{0,15},{1,0},{2,1},{3,2},{4,3},{5,4},{6,5},{7,6},{8,7},{9,8},{10,9... | collective-permute-start | bytes 24584 | tf_op jit(solution)/shard_map/ppermute | solution.py:26
  45.6 7.0 %collective-permute-start.6 = (bf16[32,128]{1,0:T(8,128)(2,1)S(1)}, bf16[32,128]{1,0:T(8,128)(2,1)S(1)}, u32[]{:S(2)}, u32[]{:S(2)}) collective-permute-start(bf16[32,128]{1,0:T(8,128)(2,1)S(1)} %collective-permute-done.4), channel_id=1, source_target_pairs={{0,1},{1,2},{2,3},{3,4},{4,5},{5,6},{6,7},{7,8},{8,9},{9,10},{10,1... | collective-permute-start | bytes 24584 | tf_op jit(solution)/shard_map/ppermute | solution.py:21
  45.6 7.0 %collective-permute-start.7 = (bf16[32,128]{1,0:T(8,128)(2,1)S(1)}, bf16[32,128]{1,0:T(8,128)(2,1)S(1)}, u32[]{:S(2)}, u32[]{:S(2)}) collective-permute-start(bf16[32,128]{1,0:T(8,128)(2,1)S(1)} %collective-permute-done.5), channel_id=1, source_target_pairs={{0,15},{1,0},{2,1},{3,2},{4,3},{5,4},{6,5},{7,6},{8,7},{9,8},{10,9... | collective-permute-start | bytes 24584 | tf_op jit(solution)/shard_map/ppermute | solution.py:26
  52.5 7.0 %collective-permute-start.8 = (bf16[32,128]{1,0:T(8,128)(2,1)S(1)}, bf16[32,128]{1,0:T(8,128)(2,1)S(1)}, u32[]{:S(2)}, u32[]{:S(2)}) collective-permute-start(bf16[32,128]{1,0:T(8,128)(2,1)S(1)} %collective-permute-done.6), channel_id=1, source_target_pairs={{0,1},{1,2},{2,3},{3,4},{4,5},{5,6},{6,7},{7,8},{8,9},{9,10},{10,1... | collective-permute-start | bytes 24584 | tf_op jit(solution)/shard_map/ppermute | solution.py:21
  52.5 7.0 %collective-permute-start.9 = (bf16[32,128]{1,0:T(8,128)(2,1)S(1)}, bf16[32,128]{1,0:T(8,128)(2,1)S(1)}, u32[]{:S(2)}, u32[]{:S(2)}) collective-permute-start(bf16[32,128]{1,0:T(8,128)(2,1)S(1)} %collective-permute-done.7), channel_id=1, source_target_pairs={{0,15},{1,0},{2,1},{3,2},{4,3},{5,4},{6,5},{7,6},{8,7},{9,8},{10,9... | collective-permute-start | bytes 24584 | tf_op jit(solution)/shard_map/ppermute | solution.py:26
  59.5 7.0 %collective-permute-start.10 = (bf16[32,128]{1,0:T(8,128)(2,1)S(1)}, bf16[32,128]{1,0:T(8,128)(2,1)S(1)}, u32[]{:S(2)}, u32[]{:S(2)}) collective-permute-start(bf16[32,128]{1,0:T(8,128)(2,1)S(1)} %collective-permute-done.8), channel_id=1, source_target_pairs={{0,1},{1,2},{2,3},{3,4},{4,5},{5,6},{6,7},{7,8},{8,9},{9,10},{10,1... | collective-permute-start | bytes 24584 | tf_op jit(solution)/shard_map/ppermute | solution.py:21
  59.5 7.0 %collective-permute-start.11 = (bf16[32,128]{1,0:T(8,128)(2,1)S(1)}, bf16[32,128]{1,0:T(8,128)(2,1)S(1)}, u32[]{:S(2)}, u32[]{:S(2)}) collective-permute-start(bf16[32,128]{1,0:T(8,128)(2,1)S(1)} %collective-permute-done.9), channel_id=1, source_target_pairs={{0,15},{1,0},{2,1},{3,2},{4,3},{5,4},{6,5},{7,6},{8,7},{9,8},{10,9... | collective-permute-start | bytes 24584 | tf_op jit(solution)/shard_map/ppermute | solution.py:26
  66.5 7.0 %collective-permute-start.12 = (bf16[32,128]{1,0:T(8,128)(2,1)S(1)}, bf16[32,128]{1,0:T(8,128)(2,1)S(1)}, u32[]{:S(2)}, u32[]{:S(2)}) collective-permute-start(bf16[32,128]{1,0:T(8,128)(2,1)S(1)} %collective-permute-done.10), channel_id=1, source_target_pairs={{0,1},{1,2},{2,3},{3,4},{4,5},{5,6},{6,7},{7,8},{8,9},{9,10},{10,1... | collective-permute-start | bytes 24584 | tf_op jit(solution)/shard_map/ppermute | solution.py:21
  66.5 7.0 %collective-permute-start.13 = (bf16[32,128]{1,0:T(8,128)(2,1)S(1)}, bf16[32,128]{1,0:T(8,128)(2,1)S(1)}, u32[]{:S(2)}, u32[]{:S(2)}) collective-permute-start(bf16[32,128]{1,0:T(8,128)(2,1)S(1)} %collective-permute-done.11), channel_id=1, source_target_pairs={{0,15},{1,0},{2,1},{3,2},{4,3},{5,4},{6,5},{7,6},{8,7},{9,8},{10,9... | collective-permute-start | bytes 24584 | tf_op jit(solution)/shard_map/ppermute | solution.py:26
  73.4 7.0 %collective-permute-start.14 = (bf16[32,128]{1,0:T(8,128)(2,1)S(1)}, bf16[32,128]{1,0:T(8,128)(2,1)S(1)}, u32[]{:S(2)}, u32[]{:S(2)}) collective-permute-start(bf16[32,128]{1,0:T(8,128)(2,1)S(1)} %collective-permute-done.12), channel_id=1, source_target_pairs={{0,1},{1,2},{2,3},{3,4},{4,5},{5,6},{6,7},{7,8},{8,9},{9,10},{10,1... | collective-permute-start | bytes 24584 | tf_op jit(solution)/shard_map/ppermute | solution.py:21
  116.1 1.0 copy-start
Sparse Core Ops, SparseCore 0:
  117.3 75.5 reduce-scatter.1
